TPU v7x, 512 devices: a whole 4x4x16 slice. The times are simulated.
512 devices in a mesh: blk: 32 (over x, y, z_hi), rel: 16 (over z_lo, core).
Axes of the slice: x: 4, y: 4, z: 16 (z_hi: 2, z_lo: 8; z = z_hi * 8 + z_lo), core: 2. Of those that a mesh axis runs over, the one named last changes fastest.
Arguments:
- features: bfloat16 [16384, 512], P(('blk', 'rel')), may hold values from -6 to 6
- adjacency: int32 [6, 512, 16, 1024], P(None, 'blk', 'rel'), may hold values from -2147483648 to 2147483646, as said below
- tile_mask: int32 [6, 128, 32, 16], P(None, 'blk', None, 'rel'), may hold values from 0 to 1
- bases: bfloat16 [512, 8, 512], P('rel'), may hold values from -0.25 to 0.25
- coefficients: float32 [6, 8], replicated, may hold values from -2 to 2
- self_weight: bfloat16 [512, 512], P('rel'), may hold values from -0.25 to 0.25
Outputs:
- updated: bfloat16 [16384, 512], P(('blk', 'rel'))
Inputs may be any that keep to these rules, and one draw needn't show every extreme that they name: `adjacency`: each word holds 32 edge bits, bit t for destination node 32 * word index + t.
All inputs are finite; a program needn't handle non-finite values.
Results may differ from a plain program's by a relative error of at most 0.0058.
Values may be sent and summed in bfloat16 or wider, within the bound.
A program may use at most 64 MiB of HBM per device.

v0:
```python
import jax
import jax.numpy as jnp
from jax import lax
from jax.sharding import Mesh
from jax.sharding import PartitionSpec as P

BLK = ("blk_0", "blk_1", "blk_2")
BLK_REL = ("blk_0", "blk_1", "blk_2", "rel")


def in_order(tiles, dim):
    shape = list(tiles.shape[1:])
    shape[dim] *= tiles.shape[0]
    return jnp.moveaxis(tiles, 0, dim).reshape(shape)


def gather_in_order(x, axes, turns):
    tiles = x
    for k in turns:
        tiles = lax.all_gather(tiles, axes[k])
    done = turns[::-1]
    back = [done.index(k) for k in range(len(axes))]
    tiles = tiles.transpose(*back, *range(len(axes), tiles.ndim))
    return tiles.reshape(-1, *x.shape)


def whole_of(x, axes, turns, dim):
    return in_order(gather_in_order(x, axes, turns), dim)


def split_up(x, dim, devices):
    shape = x.shape
    tiles = x.reshape(*shape[:dim], devices, shape[dim] // devices, *shape[dim + 1 :])
    return jnp.moveaxis(tiles, dim, 0)


def sum_at_owner(x, axis, dim):
    tiles = split_up(x, dim, lax.axis_size(axis))
    arrived = lax.all_to_all(tiles, axis, split_axis=0, concat_axis=0, tiled=True)
    return arrived.astype(jnp.float32).sum(axis=0)


def in_one_piece(arrays, axis, dim, along):
    columns = [a.reshape(*a.shape[:along], -1) for a in arrays]
    both = jnp.concatenate(columns, axis=along)
    whole, at, finished = (sum_at_owner(both, axis, dim), 0, [])
    for a, column in zip(arrays, columns):
        share = whole[..., at : at + column.shape[along]]
        finished.append(share.reshape(*share.shape[:along], *a.shape[along:]))
        at += column.shape[along]
    return tuple(finished)


def expand_edges(packed, tile_flags):
    shifts = jnp.arange(32, dtype=jnp.int32)
    edge_bits = jnp.bitwise_and(
        jnp.right_shift(packed[:, :, None, :], shifts[None, None, :, None]), 1
    )
    edge_bits = edge_bits.reshape(packed.shape[0], packed.shape[1] * 32, packed.shape[2])
    tile_rows = jnp.repeat(tile_flags, 128, axis=1)
    return edge_bits * tile_rows


def shards(features, adjacency, tile_mask, bases, coefficients, self_weight):
    relations = adjacency.shape[0]
    words = adjacency.shape[1]
    blocks = tile_mask.shape[2]
    sub_rows = features.shape[0]
    width = features.shape[1]
    own_rows = jnp.einsum(
        "rb,ibj->irj", coefficients, bases.astype(jnp.float32), precision=lax.Precision.HIGHEST
    ).astype(jnp.bfloat16)
    rel_weight, self_full = (
        lax.all_gather(own_rows, "rel", axis=0, tiled=True),
        lax.all_gather(self_weight, "rel", axis=0, tiled=True),
    )
    weight_all = rel_weight.reshape(width, relations * width)
    packed_all = adjacency.reshape(relations, words, blocks * sub_rows)
    flags_all = jnp.repeat(
        tile_mask.reshape(relations, tile_mask.shape[1], blocks), sub_rows, axis=2
    )
    portion = whole_of(features, BLK, (2, 0, 1), 0)
    values = jnp.dot(portion, weight_all, preferred_element_type=jnp.float32).astype(jnp.bfloat16)
    aggregate_values = values.reshape(portion.shape[0], relations, width)
    edges = expand_edges(packed_all, flags_all)
    degree = jnp.sum(edges, axis=(0, 2)).astype(jnp.float32)
    edges = edges.astype(jnp.bfloat16)
    running = jnp.einsum("rns,srd->nd", edges, aggregate_values, preferred_element_type=jnp.float32)
    message, degree = (running, degree)
    message, degree = in_one_piece(
        (message.astype(jnp.bfloat16), degree.astype(jnp.bfloat16)), "rel", 0, 1
    )
    own = jnp.dot(features, self_full, preferred_element_type=jnp.float32)
    return jax.nn.relu(own + message * lax.rsqrt(1.0 + degree)[:, None]).astype(jnp.bfloat16)


def solution(mesh):
    torus = Mesh(
        mesh.devices.reshape(4, 4, 2, mesh.shape["rel"]), ("blk_0", "blk_1", "blk_2", "rel")
    )
    placed = (
        P(BLK_REL, None),
        P(None, BLK, "rel", None),
        P(None, BLK, None, "rel"),
        P("rel", None, None),
        P(),
        P("rel", None),
    )
    return jax.shard_map(
        shards, mesh=torus, in_specs=placed, out_specs=P(BLK_REL, None), check_vma=False
    )
```

profile of v0, /device:TPU:1, one launch (start us, length us, event | category | flops | bytes accessed | tf_op | source)
XLA Modules:
  0.0 253.5 jit_solution(931051646286977591)
XLA Ops:
  6.5 16.8 %all-gather = bf16[64,512]{1,0:T(8,128)(2,1)S(1)} all-gather(bf16[32,512]{1,0:T(8,128)(2,1)} %param.6), channel_id=2, replica_groups=mesh['blk_0'=4,'blk_1'=4,'blk_2'=2,'rel'=16] {'blk_2'}, dimensions={0}, use_global_device_ids=true | all-gather | bytes 98304 | tf_op jit(solution)/shard_map/all_gather | solution.py:20
  23.3 11.4 %all-gather.1 = bf16[8,32,512]{2,1,0:T(8,128)(2,1)} all-gather(bf16[2,32,512]{2,1,0:T(8,128)(2,1)S(1)} %bitcast.54), channel_id=3, replica_groups=mesh['blk_0'=4,'blk_1'=4,'blk_2'=2,'rel'=16] {'blk_0'}, dimensions={0}, use_global_device_ids=true | all-gather | bytes 327680 | tf_op jit(solution)/shard_map/all_gather | solution.py:20
  34.8 1.0 fusion.3
  35.9 0.7 copy.15
  36.8 1.1 copy.23
  37.8 0.9 broadcast_in_dim.14
  38.7 0.2 reshape.48
  38.9 0.1 broadcast_in_dim.16
  39.0 0.1 broadcast_in_dim.17
  39.1 2.2 multiply_reduce_fusion
  41.4 0.2 copy.19
  41.6 5.2 %fusion = bf16[6,512,1024]{2,1,0:T(8,128)(2,1)} fusion(s32[6,4,1024]{2,1,0:T(4,128)S(1)} %reshape.48, s32[512]{0:T(512)S(1)} %shift_right_arithmetic.32, s32[6,16,1024]{2,1,0:T(8,128)S(1)} %bitcast.48), kind=kLoop, calls=%fused_computation.1 | loop fusion | flops 12582912 | bytes 6785024 | tf_op jit(solution)/shard_map/convert_element_type | solution.py:87
  46.8 21.6 %all-gather.8.cloned.1.call-done = bf16[16,2,32,512]{3,2,1,0:T(8,128)(2,1)} async-done(((bf16[4,2,32,512]{3,2,1,0:T(8,128)(2,1)}), bf16[16,2,32,512]{3,2,1,0:T(8,128)(2,1)}) %all-gather.8.cloned.1.call-update) | async-done | bytes 1048592 | tf_op jit(solution)/shard_map/all_gather | solution.py:20
  68.4 1.3 copy.17
  69.7 105.3 %all-gather.6.cloned.1.call-done = bf16[512,6,512]{2,0,1:T(8,128)(2,1)} async-done(((bf16[32,6,512]{2,0,1:T(8,128)(2,1)}), bf16[512,6,512]{2,0,1:T(8,128)(2,1)}) %all-gather.6.cloned.1.call-update) | async-done | bytes 3145744 | tf_op jit(solution)/shard_map/all_gather | solution.py:74
  175.0 4.8 %copy.16 = bf16[512,6,512]{0,2,1:T(8,128)(2,1)} copy(bf16[512,6,512]{2,0,1:T(8,128)(2,1)} %all-gather.6.cloned.1.call-done) | data formatting | bytes 6291456 | tf_op jit(solution)/shard_map/all_gather | solution.py:74
  179.8 5.7 %convolution_convert_fusion = bf16[3072,1024]{1,0:T(8,128)(2,1)S(1)} fusion(bf16[512,3072]{0,1:T(8,128)(2,1)} %bitcast.49, bf16[1024,512]{1,0:T(8,128)(2,1)S(1)} %bitcast.52), kind=kOutput, calls=%fused_computation.5 | convolution fusion | flops 3224371200 | bytes 10485760 | tf_op jit(solution)/shard_map/dot_general | solution.py:83
  185.6 3.4 %fusion.2 = bf16[512,512]{1,0:T(8,128)(2,1)S(1)} fusion(bf16[6,512,1024]{2,1,0:T(8,128)(2,1)S(1)} %bitcast.46, bf16[1024,6,512]{0,2,1:T(8,128)(2,1)S(1)} %bitcast.56), kind=kOutput, calls=%fused_computation.8 | convolution fusion | flops 3221487616 | bytes 13107200 | tf_op jit(solution)/shard_map/rns,srd->nd/dot_general | solution.py:88
  189.1 0.9 pad_maximum_fusion
  190.0 10.5 %all-to-all-start = ((bf16[16,32,513]{2,1,0:T(8,128)(2,1)}), bf16[16,32,513]{2,1,0:T(8,128)(2,1)S(1)}, u32[]{:S(2)}, u32[]{:S(2)}) async-start(bf16[16,32,513]{2,1,0:T(8,128)(2,1)} %pad_maximum_fusion), calls=%async_computation | async-start | bytes 1310720 | tf_op jit(solution)/shard_map/all_to_all | solution.py:39
  200.5 45.1 %all_gather.24 = bf16[512,512]{1,0:T(8,128)(2,1)S(1)} all-gather(bf16[32,512]{1,0:T(8,128)(2,1)S(1)} %copy-done.2), channel_id=1, replica_groups=mesh['blk_0'=4,'blk_1'=4,'blk_2'=2,'rel'=16] {'rel'}, dimensions={0}, use_global_device_ids=true | all-gather | bytes 557056 | tf_op jit(solution)/shard_map/all_gather | solution.py:75
  245.6 0.1 convert_reduce_fusion
  245.7 0.1 fusion.7
  245.8 0.8 fusion.5
  (19 shorter events, 0.2 us)
Async XLA Ops:
  6.5 28.3 %copy-start = (bf16[32,8,512]{2,1,0:T(8,128)(2,1)S(1)}, bf16[32,8,512]{2,1,0:T(8,128)(2,1)}, u32[]{:S(2)}) copy-start(bf16[32,8,512]{2,1,0:T(8,128)(2,1)} %param.9) | copy-start | bytes 786436
  6.5 61.9 %all-gather.8.cloned.1.call-start = ((), (), s32[]{:S(2)}) async-start(), calls=%async_computation.2 | async-start | bytes 1310720 | tf_op jit(solution)/shard_map/all_gather | solution.py:20
  34.8 140.2 %all-gather.6.cloned.1.call-start = ((), (), s32[]{:S(2)}) async-start(), calls=%async_computation.1 | async-start | bytes 3342336 | tf_op jit(solution)/shard_map/all_gather | solution.py:74
  175.0 10.6 %slice-start = ((s8[6291456]{0:T(1024)(128)(4,1)}), s8[2097152]{0:T(1024)(128)(4,1)S(1)}, s32[]{:S(2)}) async-start(s8[6291456]{0:T(1024)(128)(4,1)} %bitcast.45), calls=%async_computation.3 | async-start | bytes 4194304
  179.8 5.7 %slice-start.1 = ((s8[6291456]{0:T(1024)(128)(4,1)}), s8[4194304]{0:T(1024)(128)(4,1)S(1)}, s32[]{:S(2)}) async-start(s8[6291456]{0:T(1024)(128)(4,1)} %bitcast.45), calls=%async_computation.4 | async-start | bytes 8388608
  185.6 14.8 %copy-start.2 = (bf16[32,512]{1,0:T(8,128)(2,1)S(1)}, bf16[32,512]{1,0:T(8,128)(2,1)}, u32[]{:S(2)}) copy-start(bf16[32,512]{1,0:T(8,128)(2,1)} %param.11) | copy-start | bytes 98308
  185.6 60.2 %copy-start.1 = (bf16[32,512]{1,0:T(8,128)(2,1)S(1)}, bf16[32,512]{1,0:T(8,128)(2,1)}, u32[]{:S(2)}) copy-start(bf16[32,512]{1,0:T(8,128)(2,1)} %param.6) | copy-start | bytes 98308
  190.0 55.6 %all-to-all-start = ((bf16[16,32,513]{2,1,0:T(8,128)(2,1)}), bf16[16,32,513]{2,1,0:T(8,128)(2,1)S(1)}, u32[]{:S(2)}, u32[]{:S(2)}) async-start(bf16[16,32,513]{2,1,0:T(8,128)(2,1)} %pad_maximum_fusion), calls=%async_computation | async-start | bytes 1310720 | tf_op jit(solution)/shard_map/all_to_all | solution.py:39
Sparse Core Ops, SparseCore 0:
  34.9 33.4 all-gather.7
  70.5 104.4 all-gather.5
where the time goes:
time: 254 us; the launch traced here: 253 us
  waiting for transfers between devices  127 us (50%)
  blocking collectives  73.3 us (29%)
  between operations  13.5 us (5%)
  matrix products  11 us (4%)
  starting transfers between devices  10.5 us (4%)
  local copies, waits for them, and re-layouts  9.54 us (4%)
  other arithmetic  8.61 us (3%)
    all_gather x1, waiting for transfers between devices, shards(): lax.all_gather(own_rows, 'rel', axis=0, tiled=True)  105 us
    all_gather x1, blocking collectives, shards(): lax.all_gather(self_weight, 'rel', axis=0, tiled=True)  45.1 us
    all_gather x2, blocking collectives, gather_in_order(): tiles = lax.all_gather(tiles, axes[k])  28.2 us
    all_gather x1, waiting for transfers between devices, gather_in_order(): tiles = lax.all_gather(tiles, axes[k])  21.6 us
    all_to_all x1, starting transfers between devices, sum_at_owner(): lax.all_to_all(tiles, axis, split_axis=0, concat_axis=0, tiled=True)  10.5 us
    dot_general x1, matrix products, shards(): jnp.dot(portion, weight_all, preferred_element_type=jnp.float32)  5.73 us
    convert_element_type x1, other arithmetic, shards(): edges = edges.astype(jnp.bfloat16)  5.23 us
  transfers between devices with their start and end apart: 3, of which 2 were waited for; matrix products, arithmetic and copies ran while one was open for 5% of the time, Pallas kernels for 0%

commit v1 on v0

v1 whole, which is shorter than its diff:
```python
import jax
import jax.numpy as jnp
from jax import lax
from jax.experimental import pallas as pl
from jax.experimental.pallas import tpu as pltpu
from jax.sharding import Mesh
from jax.sharding import PartitionSpec as P

AXES = ("x", "y", "h", "z", "p")
BLK = ("x", "y", "h")
REL = ("z", "p")
F32 = jnp.float32
BF16 = jnp.bfloat16
MESH = pl.DeviceIdType.MESH
SHIFTS = (1, -1, 2, -2, 3, -3, 4)


def kernel(feat_hbm, adj_hbm, mask_hbm, bases_hbm, coef, self_hbm, out_ref,
           feats, adj, mask, bases, own_self, weights, words, flags, edges, partial, counts,
           transit, deg_mine, deg_pair, deg_sum, deg_all, total, pair_out, pair_in, level_out, level_in,
           cross_out, cross_in, load_sem, send_sem, recv_sem):
    x, y, h, z, p = [lax.axis_index(a) for a in AXES]
    g = h * 8 + z
    row = 2 * z + p
    q = 1 - p

    def along_z(d):
        t = lax.rem(g + d + 16, 16)
        return (x, y, lax.div(t, 8), lax.rem(t, 8), p)

    def mate_first(m):
        return (lax.rem(x + m * q, 4), lax.rem(y + m * p, 4), h, z, p)

    def mate_second(m):
        return (lax.rem(x + m * p, 4), lax.rem(y + m * q, 4), h, z, p)

    sibling = (x, y, h, z, q)

    def slot(half, xx, yy):
        return feats.at[half, xx, lax.rem(yy, 2) * 2 + lax.div(yy, 2)]

    loads = []
    for i, (src, dst) in enumerate((
        (bases_hbm, bases), (feat_hbm, slot(h, x, y)), (self_hbm, own_self),
        (adj_hbm, adj), (mask_hbm, mask),
    )):
        copy = pltpu.make_async_copy(src, dst, load_sem.at[i])
        copy.start()
        loads.append(copy)

    barrier = pltpu.get_barrier_semaphore()
    greeted = [sibling]
    for m in (1, 2, 3):
        greeted += [mate_first(m), mate_second(m)]
    for d in (1, 2, 3, 4):
        greeted += [along_z(d), along_z(-d)]
    for device in greeted:
        pl.semaphore_signal(barrier, inc=1, device_id=device, device_id_type=MESH)

    started = []

    def send(src, dst, device):
        k = len(started)
        copy = pltpu.make_async_remote_copy(
            src_ref=src, dst_ref=dst, send_sem=send_sem.at[k], recv_sem=recv_sem.at[k],
            device_id=device, device_id_type=MESH)
        copy.start()
        started.append(copy)
        return copy

    lane = lax.broadcasted_iota(jnp.int32, (32, 256), 1)
    line = lax.broadcasted_iota(jnp.int32, (32, 256), 0)
    basis_of = lax.rem(lane, 8)
    own_row = lax.div(lane, 8) == line
    tops, mids, lows = [], [], []
    for r in range(6):
        values = jnp.zeros((32, 256), F32)
        for b in range(8):
            values = jnp.where(basis_of == b, coef[r, b], values)
        values = jnp.where(own_row, values, 0.0)
        top = values.astype(BF16)
        rest = values - top.astype(F32)
        mid = rest.astype(BF16)
        tops.append(top)
        mids.append(mid)
        lows.append((rest - mid.astype(F32)).astype(BF16))
    loads[0].wait()
    loads[2].wait()
    rows = bases[...]
    for r in range(6):
        made = (jnp.dot(lows[r], rows, preferred_element_type=F32)
                + jnp.dot(mids[r], rows, preferred_element_type=F32)
                + jnp.dot(tops[r], rows, preferred_element_type=F32)).astype(BF16)
        for s in range(4):
            weights[s, row, r] = made[:, 128 * s:128 * s + 128]
    for s in range(4):
        weights[s, row, 6] = own_self[:, 128 * s:128 * s + 128]

    loads[3].wait()
    loads[4].wait()
    flags[...] = jnp.zeros((128, 128), F32)
    for r in range(6):
        flags[4 * r:4 * r + 4, 0:32] = mask[r].astype(F32)
    pick = (lax.div(lax.broadcasted_iota(jnp.int32, (96, 128), 0), 4)
            == lax.broadcasted_iota(jnp.int32, (96, 128), 1)).astype(BF16)
    spread = (lax.div(lax.broadcasted_iota(jnp.int32, (128, 1024), 1), 32)
              == lax.broadcasted_iota(jnp.int32, (128, 1024), 0)).astype(BF16)
    per_word = jnp.dot(pick, flags[...].astype(BF16), preferred_element_type=F32).astype(BF16)
    keep = jnp.dot(per_word, spread, preferred_element_type=F32)
    odd = lax.rem(lax.div(lax.broadcasted_iota(jnp.int32, (16, 128), 1), 32), 2) == 1
    for r in range(6):
        for c in range(4):
            at = 256 * c
            first = jnp.where(keep[16 * r:16 * r + 16, at:at + 128] > 0.5, adj[r, :, 0, at:at + 128], 0)
            second = jnp.where(keep[16 * r:16 * r + 16, at + 128:at + 256] > 0.5, adj[r, :, 0, at + 128:at + 256], 0)
            words[0, r, :, 128 * c:128 * c + 128] = jnp.where(odd, pltpu.roll(second, 32, 1), first)
            words[1, r, :, 128 * c:128 * c + 128] = jnp.where(odd, second, pltpu.roll(first, 96, 1))
    counts[...] = jnp.zeros((512, 128), jnp.int32)
    loads[1].wait()

    pl.semaphore_wait(barrier, len(greeted))

    mine = slot(h, x, y)
    hop_a = send(mine.at[0:16], transit.at[0], along_z(4))
    hop_b = send(mine.at[16:32], transit.at[1], along_z(-4))
    own_first = [send(mine, mine, mate_first(m)) for m in (1, 2, 3)]
    quarter = x * q + y * p
    z_copies = []
    for d in SHIFTS:
        shift = d if d != 4 else 4 - 8 * p
        z_copies.append(send(weights.at[quarter, row], weights.at[quarter, row], along_z(shift)))
    pair_copies = [send(weights.at[s, row], weights.at[s, row], sibling) for s in range(4)]

    def expand(half):
        shifts = lax.broadcasted_iota(jnp.int32, (32, 512), 0)

        def one(r, carry):
            packed = words[half, r]
            for w in range(16):
                bits = jnp.bitwise_and(jnp.right_shift(jnp.broadcast_to(packed[w:w + 1, :], (32, 512)), shifts), 1)
                edges[half, r, 32 * w:32 * w + 32, :] = bits.astype(F32).astype(BF16)
                counts[32 * w:32 * w + 32, :] += (
                    (bits[:, 0:128] + bits[:, 128:256]) + (bits[:, 256:384] + bits[:, 384:512]))
            return carry

        lax.fori_loop(0, 6, one, 0)

    def second_turn(half, first):
        sent = []
        for m in (0, 1, 2, 3):
            if m:
                first[m - 1].wait_recv()
            part = slot(half, lax.rem(x - m * q + 4, 4), lax.rem(y - m * p + 4, 4))
            sent += [send(part, part, mate_second(k)) for k in (1, 2, 3)]
        return sent

    expand(h)
    own_second = second_turn(h, own_first)
    hop_a.wait_recv()
    behind = lax.div(lax.rem(g + 12, 16), 8)
    end_a = send(transit.at[0], slot(behind, x, y).at[0:16], along_z(4))
    hop_b.wait_recv()
    ahead = lax.div(lax.rem(g + 4, 16), 8)
    end_b = send(transit.at[1], slot(ahead, x, y).at[16:32], along_z(-4))

    xy_copies = []

    def forward_z(k):
        d = SHIFTS[k]
        z_copies[k].wait_recv()
        shift = d if d != 4 else 4 - 8 * p
        source = lax.rem(lax.rem(g - shift + 16, 16), 8) * 2 + p
        part = weights.at[quarter, source]
        xy_copies.append([(m, source, send(part, part, mate_first(m))) for m in (1, 2, 3)])
        pair_copies.append(send(part, part, sibling))

    def forward_xy(k):
        for m, source, copy in xy_copies[k]:
            copy.wait_recv()
            part = weights.at[lax.rem(quarter - m + 4, 4), source]
            pair_copies.append(send(part, part, sibling))

    other = 1 - h
    expand(other)
    forward_z(0)
    forward_z(1)

    ones = jnp.ones((8, 128), BF16)
    for c in range(4):
        deg_mine[c] = lax.dot_general(
            ones, counts[128 * c:128 * c + 128, :].astype(F32).astype(BF16), (((1,), (1,)), ((), ())),
            preferred_element_type=F32)
    deg_copy = send(deg_mine, deg_pair, sibling)

    for copy in own_second:
        copy.wait_recv()
    held = feats[h].reshape(512, 512)
    for r in range(6):
        partial[r] = jnp.dot(edges[h, r], held, preferred_element_type=F32)
    forward_z(2)
    forward_z(3)
    deg_copy.wait_recv()
    deg_sum[...] = deg_mine[...] + deg_pair[...]
    deg_copies = []
    for m in range(1, 8):
        zz = lax.rem(z + m, 8)
        deg_copies.append(send(deg_sum.at[lax.div(zz, 2)], deg_all.at[m], (x, y, h, zz, p)))
    deg_all[0] = deg_sum[lax.div(z, 2)]

    end_a.wait_recv()
    end_b.wait_recv()
    far = slot(other, x, y)
    far_first = [send(far, far, mate_first(m)) for m in (1, 2, 3)]
    forward_z(4)
    forward_z(5)
    far_second = second_turn(other, far_first)
    forward_z(6)
    for k in range(7):
        forward_xy(k)
    for copy in far_second:
        copy.wait_recv()
    for copy in pair_copies:
        copy.wait_recv()

    far_held = feats[other].reshape(512, 512)

    def weight(r):
        return jnp.concatenate([weights[s, :, r].reshape(512, 128) for s in range(4)], axis=1)

    side = lax.div(z, 4)
    place = lax.rem(z, 4)

    def group(turn, which):
        at = pl.ds(pl.multiple_of(which * 256, 256), 256)
        for r in range(6):
            a = (partial[r, at, :] + jnp.dot(edges[other, r, at, :], far_held, preferred_element_type=F32)).astype(BF16)
            term = jnp.dot(a, weight(r), preferred_element_type=F32).reshape(4, 2, 32, 512)
            if r == 0:
                total[turn] = term
            else:
                total[turn] += term
        pair_out[turn] = total[turn, :, q].astype(BF16)
        pair = send(pair_out.at[turn], pair_in.at[turn], sibling)
        return pair

    def level_sends(turn, pair):
        pair.wait_recv()
        total[turn, :, p] += pair_in[turn].astype(F32)
        level_out[turn] = total[turn, :, p].astype(BF16)
        sent = []
        for m in (1, 2, 3):
            i = lax.rem(place + m, 4)
            sent.append(send(level_out.at[turn, i], level_in.at[turn, m - 1], (x, y, h, side * 4 + i, p)))
        return sent

    def level_sum(turn, sent):
        for copy in sent:
            copy.wait_recv()
        value = total[turn, place, p]
        for m in range(3):
            value += level_in[turn, m].astype(F32)
        return value

    pair_far = group(0, 1 - side)
    level_far = level_sends(0, pair_far)
    pair_near = group(1, side)
    cross_out[...] = level_sum(0, level_far).astype(BF16)
    cross = send(cross_out, cross_in, (x, y, h, (1 - side) * 4 + place, p))
    level_near = level_sends(1, pair_near)

    own = jnp.dot(mine[...], weight(6), preferred_element_type=F32)
    for copy in deg_copies:
        copy.wait_recv()
    degrees = deg_all[0]
    for m in range(1, 8):
        degrees += deg_all[m]
    place_of = (lax.broadcasted_iota(jnp.int32, (32, 128), 1)
                == lax.rem(row, 4) * 32 + lax.broadcasted_iota(jnp.int32, (32, 128), 0))
    degree = jnp.sum(jnp.where(place_of, jnp.broadcast_to(degrees[0:1, :], (32, 128)), 0.0), axis=1, keepdims=True)
    scale = lax.rsqrt(1.0 + degree)
    message = level_sum(1, level_near)
    cross.wait_recv()
    message += cross_in[...].astype(F32)
    out_ref[...] = jnp.maximum(own + message * scale, 0.0).astype(BF16)
    for copy in started:
        copy.wait_send()


def shards(features, adjacency, tile_mask, bases, coefficients, self_weight):
    hbm = pl.BlockSpec(memory_space=pltpu.HBM)
    n = 160
    return pl.pallas_call(
        kernel,
        out_shape=jax.ShapeDtypeStruct((32, 512), BF16),
        in_specs=[hbm, hbm, hbm, hbm, pl.BlockSpec(memory_space=pltpu.SMEM), hbm],
        out_specs=pl.BlockSpec(memory_space=pltpu.VMEM),
        scratch_shapes=[
            pltpu.VMEM((2, 4, 4, 32, 512), BF16),
            pltpu.VMEM((6, 16, 1, 1024), jnp.int32),
            pltpu.VMEM((6, 4, 32), jnp.int32),
            pltpu.VMEM((256, 512), BF16),
            pltpu.VMEM((32, 512), BF16),
            pltpu.VMEM((4, 16, 7, 32, 128), BF16),
            pltpu.VMEM((2, 6, 16, 512), jnp.int32),
            pltpu.VMEM((128, 128), F32),
            pltpu.VMEM((2, 6, 512, 512), BF16),
            pltpu.VMEM((6, 512, 512), F32),
            pltpu.VMEM((512, 128), jnp.int32),
            pltpu.VMEM((2, 16, 512), BF16),
            pltpu.VMEM((4, 8, 128), F32),
            pltpu.VMEM((4, 8, 128), F32),
            pltpu.VMEM((4, 8, 128), F32),
            pltpu.VMEM((8, 8, 128), F32),
            pltpu.VMEM((2, 4, 2, 32, 512), F32),
            pltpu.VMEM((2, 4, 32, 512), BF16),
            pltpu.VMEM((2, 4, 32, 512), BF16),
            pltpu.VMEM((2, 4, 32, 512), BF16),
            pltpu.VMEM((2, 3, 32, 512), BF16),
            pltpu.VMEM((32, 512), BF16),
            pltpu.VMEM((32, 512), BF16),
            pltpu.SemaphoreType.DMA((5,)),
            pltpu.SemaphoreType.DMA((n,)),
            pltpu.SemaphoreType.DMA((n,)),
        ],
        compiler_params=pltpu.CompilerParams(
            collective_id=0, has_side_effects=True, vmem_limit_bytes=56 * 1024 * 1024),
    )(features, adjacency, tile_mask.reshape(6, 4, 32), bases.reshape(256, 512), coefficients, self_weight)


def solution(mesh):
    torus = Mesh(mesh.devices.reshape(4, 4, 2, 8, 2), AXES)
    placed = (
        P(AXES, None),
        P(None, BLK, REL, None),
        P(None, BLK, None, REL),
        P(REL, None, None),
        P(),
        P(REL, None),
    )
    return jax.shard_map(
        shards, mesh=torus, in_specs=placed, out_specs=P(AXES, None), check_vma=False
    )
```

time: 254 us -> 60.1 us (0.24)
  waiting for transfers between devices: 127 us -> 0 us
  blocking collectives: 73.3 us -> 0 us
  Pallas kernels: 0 us -> 58.5 us
  between operations: 13.5 us -> 0.01 us
  matrix products: 11 us -> 0 us
  starting transfers between devices: 10.5 us -> 0 us
  other arithmetic: 8.61 us -> 0 us
  local copies, waits for them, and re-layouts: 9.54 us -> 1.38 us
    all_gather x2 -> x0, waiting for transfers between devices: 127 us -> none  [the longest x1 105 us: shards(): lax.all_gather(own_rows, 'rel', axis=0, tiled=True)]
    all_gather x3 -> x0, blocking collectives: 73.3 us -> none  [the longest x1 45.1 us: shards(): lax.all_gather(self_weight, 'rel', axis=0, tiled=True)]
    pallas_call x0 -> x1, Pallas kernels: none -> 58.5 us  [shards(): pl.pallas_call(kernel, out_shape=jax.ShapeDtypeStruct((32, 512), BF16), i...]
    dot_general x4 -> x0, matrix products: 11 us -> none  [the longest x1 5.73 us: shards(): jnp.dot(portion, weight_all, preferred_element_type=jnp.float32)]
    all_to_all x1 -> x0, starting transfers between devices: 10.5 us -> none  [sum_at_owner(): lax.all_to_all(tiles, axis, split_axis=0, concat_axis=0, tiled=True)]
    convert_element_type x2 -> x0, other arithmetic: 5.24 us -> none  [the longest x1 5.23 us: shards(): edges = edges.astype(jnp.bfloat16)]
    all_gather x1 -> x0, local copies, waits for them, and re-layouts: 4.82 us -> none  [shards(): lax.all_gather(own_rows, 'rel', axis=0, tiled=True)]
  transfers between devices with their start and end apart: 3 -> 0, of which waited for: 2 -> 0; matrix products, arithmetic and copies ran while one was open for 5% -> 0% of each run, Pallas kernels for 0% -> 0%
where the time goes in v1:
time: 60.1 us; the launch traced here: 59.9 us
  Pallas kernels  58.5 us (97%)
  local copies, waits for them, and re-layouts  1.38 us (2%)
    pallas_call x1, Pallas kernels, shards(): pl.pallas_call(kernel, out_shape=jax.ShapeDtypeStruct((32, 512), BF16), i...  58.5 us
    unnamed x1, local copies, waits for them, and re-layouts  1.38 us

profile of v1, /device:TPU:1, one launch (start us, length us, event | category | flops | bytes accessed | tf_op | source)
XLA Modules:
  0.0 59.9 jit_solution(12212689533288940245)
XLA Ops:
  0.0 58.5 %shard_map.64 = bf16[32,512]{1,0:T(8,128)(2,1)} custom-call(bf16[32,512]{1,0:T(8,128)(2,1)} %feat_hbm.1, s32[6,16,1,1024]{3,2,1,0:T(1,128)} %adj_hbm.1, s32[6,4,32]{2,1,0:T(4,128)} %bitcast.3, bf16[256,512]{1,0:T(8,128)(2,1)} %bitcast.2, f32[6,8]{1,0:T(8,128)} %coef.1, bf16[32,512]{1,0:T(8,128)(2,1)} %self_hbm.1), custom_call_target="tpu_custom_call" | custom-call | tf_op jit(solution)/shard_map/pallas_call | solution.py:292
  58.5 1.4 %copy.8 = bf16[32,512]{1,0:T(8,128)(2,1)} copy(bf16[32,512]{1,0:T(8,128)(2,1)} %shard_map.64) | data formatting | bytes 65536

commit v2 on v1

--- a/solution.py
+++ b/solution.py
@@ -15,8 +15,8 @@
 SHIFTS = (1, -1, 2, -2, 3, -3, 4)
 
 
-def kernel(feat_hbm, adj_hbm, mask_hbm, bases_hbm, coef, self_hbm, out_ref,
-           feats, adj, mask, bases, own_self, weights, words, flags, edges, partial, counts,
+def kernel(feat_hbm, adj_hbm, mask_hbm, bases_hbm, coef_hbm, self_hbm, out_ref,
+           feats, adj, mask, bases, coef, own_self, weights, words, flags, edges, partial, counts, summed,
            transit, deg_mine, deg_pair, deg_sum, deg_all, total, pair_out, pair_in, level_out, level_in,
            cross_out, cross_in, load_sem, send_sem, recv_sem):
     x, y, h, z, p = [lax.axis_index(a) for a in AXES]
@@ -39,23 +39,23 @@
     def slot(half, xx, yy):
         return feats.at[half, xx, lax.rem(yy, 2) * 2 + lax.div(yy, 2)]
 
+    barrier = pltpu.get_barrier_semaphore()
+    greeted = [sibling]
+    for d in (4, 3, 2, 1):
+        greeted += [along_z(d), along_z(-d)]
+    for m in (2, 1, 3):
+        greeted += [mate_first(m), mate_second(m)]
+    for device in greeted:
+        pl.semaphore_signal(barrier, inc=1, device_id=device, device_id_type=MESH)
+    mine = slot(h, x, y)
     loads = []
     for i, (src, dst) in enumerate((
-        (bases_hbm, bases), (feat_hbm, slot(h, x, y)), (self_hbm, own_self),
-        (adj_hbm, adj), (mask_hbm, mask),
+        (feat_hbm, mine), (coef_hbm, coef), (bases_hbm, bases), (self_hbm, own_self),
+        (mask_hbm, mask), (adj_hbm, adj),
     )):
         copy = pltpu.make_async_copy(src, dst, load_sem.at[i])
         copy.start()
         loads.append(copy)
-
-    barrier = pltpu.get_barrier_semaphore()
-    greeted = [sibling]
-    for m in (1, 2, 3):
-        greeted += [mate_first(m), mate_second(m)]
-    for d in (1, 2, 3, 4):
-        greeted += [along_z(d), along_z(-d)]
-    for device in greeted:
-        pl.semaphore_signal(barrier, inc=1, device_id=device, device_id_type=MESH)
 
     started = []
 
@@ -68,7 +68,26 @@
         started.append(copy)
         return copy
 
+    loads[0].wait()
+    pl.semaphore_wait(barrier, len(greeted))
+    hop_a = send(mine.at[0:16], transit.at[0], along_z(4))
+    hop_b = send(mine.at[16:32], transit.at[1], along_z(-4))
+
+    def first_turn(part):
+        first = [send(part, part, mate_first(m)) for m in (2, 1, 3)]
+        return first, [send(part, part, mate_second(m)) for m in (2, 1, 3)]
+
+    def second_turn(half, first):
+        sent = []
+        for m, copy in zip((1, 3, 2), first[1:] + first[:1]):
+            copy.wait_recv()
+            part = slot(half, lax.rem(x - m * q + 4, 4), lax.rem(y - m * p + 4, 4))
+            sent += [send(part, part, mate_second(k)) for k in (2, 1, 3)]
+        return sent
+
+    own_first, own_second = first_turn(mine)
     lane = lax.broadcasted_iota(jnp.int32, (32, 256), 1)
+    loads[1].wait()
     line = lax.broadcasted_iota(jnp.int32, (32, 256), 0)
     basis_of = lax.rem(lane, 8)
     own_row = lax.div(lane, 8) == line
@@ -84,8 +103,8 @@
         tops.append(top)
         mids.append(mid)
         lows.append((rest - mid.astype(F32)).astype(BF16))
-    loads[0].wait()
     loads[2].wait()
+    loads[3].wait()
     rows = bases[...]
     for r in range(6):
         made = (jnp.dot(lows[r], rows, preferred_element_type=F32)
@@ -96,8 +115,19 @@
     for s in range(4):
         weights[s, row, 6] = own_self[:, 128 * s:128 * s + 128]
 
-    loads[3].wait()
+    quarter = x * q + y * p
+    z_copies = {}
+
+    def send_z(d):
+        shift = d if d != 4 else 4 - 8 * p
+        z_copies[d] = send(weights.at[quarter, row], weights.at[quarter, row], along_z(shift))
+
+    for d in (1, -1, 2, -2):
+        send_z(d)
+    pair_copies = [send(weights.at[s, row], weights.at[s, row], sibling) for s in range(4)]
+
     loads[4].wait()
+    loads[5].wait()
     flags[...] = jnp.zeros((128, 128), F32)
     for r in range(6):
         flags[4 * r:4 * r + 4, 0:32] = mask[r].astype(F32)
@@ -116,20 +146,6 @@
             words[0, r, :, 128 * c:128 * c + 128] = jnp.where(odd, pltpu.roll(second, 32, 1), first)
             words[1, r, :, 128 * c:128 * c + 128] = jnp.where(odd, second, pltpu.roll(first, 96, 1))
     counts[...] = jnp.zeros((512, 128), jnp.int32)
-    loads[1].wait()
-
-    pl.semaphore_wait(barrier, len(greeted))
-
-    mine = slot(h, x, y)
-    hop_a = send(mine.at[0:16], transit.at[0], along_z(4))
-    hop_b = send(mine.at[16:32], transit.at[1], along_z(-4))
-    own_first = [send(mine, mine, mate_first(m)) for m in (1, 2, 3)]
-    quarter = x * q + y * p
-    z_copies = []
-    for d in SHIFTS:
-        shift = d if d != 4 else 4 - 8 * p
-        z_copies.append(send(weights.at[quarter, row], weights.at[quarter, row], along_z(shift)))
-    pair_copies = [send(weights.at[s, row], weights.at[s, row], sibling) for s in range(4)]
 
     def expand(half):
         shifts = lax.broadcasted_iota(jnp.int32, (32, 512), 0)
@@ -145,60 +161,54 @@
 
         lax.fori_loop(0, 6, one, 0)
 
-    def second_turn(half, first):
-        sent = []
-        for m in (0, 1, 2, 3):
-            if m:
-                first[m - 1].wait_recv()
-            part = slot(half, lax.rem(x - m * q + 4, 4), lax.rem(y - m * p + 4, 4))
-            sent += [send(part, part, mate_second(k)) for k in (1, 2, 3)]
-        return sent
-
     expand(h)
-    own_second = second_turn(h, own_first)
     hop_a.wait_recv()
     behind = lax.div(lax.rem(g + 12, 16), 8)
     end_a = send(transit.at[0], slot(behind, x, y).at[0:16], along_z(4))
     hop_b.wait_recv()
     ahead = lax.div(lax.rem(g + 4, 16), 8)
     end_b = send(transit.at[1], slot(ahead, x, y).at[16:32], along_z(-4))
-
-    xy_copies = []
-
-    def forward_z(k):
-        d = SHIFTS[k]
-        z_copies[k].wait_recv()
+    for d in (3, -3, 4):
+        send_z(d)
+    own_second += second_turn(h, own_first)
+
+    xy_copies = {}
+
+    def forward_z(d):
+        z_copies[d].wait_recv()
         shift = d if d != 4 else 4 - 8 * p
         source = lax.rem(lax.rem(g - shift + 16, 16), 8) * 2 + p
         part = weights.at[quarter, source]
-        xy_copies.append([(m, source, send(part, part, mate_first(m))) for m in (1, 2, 3)])
+        xy_copies[d] = [(m, source, send(part, part, mate_first(m))) for m in (2, 1, 3)]
         pair_copies.append(send(part, part, sibling))
 
-    def forward_xy(k):
-        for m, source, copy in xy_copies[k]:
+    def forward_xy(d):
+        for m, source, copy in xy_copies[d]:
             copy.wait_recv()
             part = weights.at[lax.rem(quarter - m + 4, 4), source]
             pair_copies.append(send(part, part, sibling))
 
+    for d in (1, -1, 2, -2):
+        forward_z(d)
     other = 1 - h
     expand(other)
-    forward_z(0)
-    forward_z(1)
-
     ones = jnp.ones((8, 128), BF16)
     for c in range(4):
         deg_mine[c] = lax.dot_general(
             ones, counts[128 * c:128 * c + 128, :].astype(F32).astype(BF16), (((1,), (1,)), ((), ())),
             preferred_element_type=F32)
     deg_copy = send(deg_mine, deg_pair, sibling)
-
+    end_a.wait_recv()
+    end_b.wait_recv()
+    far_first, far_second = first_turn(slot(other, x, y))
     for copy in own_second:
         copy.wait_recv()
     held = feats[h].reshape(512, 512)
     for r in range(6):
         partial[r] = jnp.dot(edges[h, r], held, preferred_element_type=F32)
-    forward_z(2)
-    forward_z(3)
+    for d in (3, -3, 4):
+        forward_z(d)
+    far_second += second_turn(other, far_first)
     deg_copy.wait_recv()
     deg_sum[...] = deg_mine[...] + deg_pair[...]
     deg_copies = []
@@ -206,22 +216,10 @@
         zz = lax.rem(z + m, 8)
         deg_copies.append(send(deg_sum.at[lax.div(zz, 2)], deg_all.at[m], (x, y, h, zz, p)))
     deg_all[0] = deg_sum[lax.div(z, 2)]
-
-    end_a.wait_recv()
-    end_b.wait_recv()
-    far = slot(other, x, y)
-    far_first = [send(far, far, mate_first(m)) for m in (1, 2, 3)]
-    forward_z(4)
-    forward_z(5)
-    far_second = second_turn(other, far_first)
-    forward_z(6)
-    for k in range(7):
-        forward_xy(k)
+    for d in SHIFTS:
+        forward_xy(d)
     for copy in far_second:
         copy.wait_recv()
-    for copy in pair_copies:
-        copy.wait_recv()
-
     far_held = feats[other].reshape(512, 512)
 
     def weight(r):
@@ -230,26 +228,34 @@
     side = lax.div(z, 4)
     place = lax.rem(z, 4)
 
-    def group(turn, which):
+    def aggregate(turn, which):
         at = pl.ds(pl.multiple_of(which * 256, 256), 256)
         for r in range(6):
-            a = (partial[r, at, :] + jnp.dot(edges[other, r, at, :], far_held, preferred_element_type=F32)).astype(BF16)
-            term = jnp.dot(a, weight(r), preferred_element_type=F32).reshape(4, 2, 32, 512)
+            summed[turn, r] = (partial[r, at, :] + jnp.dot(
+                edges[other, r, at, :], far_held, preferred_element_type=F32)).astype(BF16)
+
+    def transform(turn):
+        for r in range(6):
+            term = jnp.dot(summed[turn, r], weight(r), preferred_element_type=F32).reshape(4, 2, 32, 512)
             if r == 0:
                 total[turn] = term
             else:
                 total[turn] += term
         pair_out[turn] = total[turn, :, q].astype(BF16)
-        pair = send(pair_out.at[turn], pair_in.at[turn], sibling)
-        return pair
+        return send(pair_out.at[turn], pair_in.at[turn], sibling)
+
+    def partner(m):
+        if m == 3:
+            return 3 - place
+        return lax.rem(place + 2, 4) if m == 2 else place + 1 - 2 * lax.rem(place, 2)
 
     def level_sends(turn, pair):
         pair.wait_recv()
         total[turn, :, p] += pair_in[turn].astype(F32)
         level_out[turn] = total[turn, :, p].astype(BF16)
         sent = []
-        for m in (1, 2, 3):
-            i = lax.rem(place + m, 4)
+        for m in (3, 2, 1):
+            i = partner(m)
             sent.append(send(level_out.at[turn, i], level_in.at[turn, m - 1], (x, y, h, side * 4 + i, p)))
         return sent
 
@@ -261,13 +267,16 @@
             value += level_in[turn, m].astype(F32)
         return value
 
-    pair_far = group(0, 1 - side)
+    aggregate(0, 1 - side)
+    for copy in pair_copies:
+        copy.wait_recv()
+    pair_far = transform(0)
+    aggregate(1, side)
     level_far = level_sends(0, pair_far)
-    pair_near = group(1, side)
+    pair_near = transform(1)
+    level_near = level_sends(1, pair_near)
     cross_out[...] = level_sum(0, level_far).astype(BF16)
     cross = send(cross_out, cross_in, (x, y, h, (1 - side) * 4 + place, p))
-    level_near = level_sends(1, pair_near)
-
     own = jnp.dot(mine[...], weight(6), preferred_element_type=F32)
     for copy in deg_copies:
         copy.wait_recv()
@@ -292,13 +301,14 @@
     return pl.pallas_call(
         kernel,
         out_shape=jax.ShapeDtypeStruct((32, 512), BF16),
-        in_specs=[hbm, hbm, hbm, hbm, pl.BlockSpec(memory_space=pltpu.SMEM), hbm],
+        in_specs=[hbm] * 6,
         out_specs=pl.BlockSpec(memory_space=pltpu.VMEM),
         scratch_shapes=[
             pltpu.VMEM((2, 4, 4, 32, 512), BF16),
             pltpu.VMEM((6, 16, 1, 1024), jnp.int32),
             pltpu.VMEM((6, 4, 32), jnp.int32),
             pltpu.VMEM((256, 512), BF16),
+            pltpu.SMEM((6, 8), F32),
             pltpu.VMEM((32, 512), BF16),
             pltpu.VMEM((4, 16, 7, 32, 128), BF16),
             pltpu.VMEM((2, 6, 16, 512), jnp.int32),
@@ -306,6 +316,7 @@
             pltpu.VMEM((2, 6, 512, 512), BF16),
             pltpu.VMEM((6, 512, 512), F32),
             pltpu.VMEM((512, 128), jnp.int32),
+            pltpu.VMEM((2, 6, 256, 512), BF16),
             pltpu.VMEM((2, 16, 512), BF16),
             pltpu.VMEM((4, 8, 128), F32),
             pltpu.VMEM((4, 8, 128), F32),
@@ -318,7 +329,7 @@
             pltpu.VMEM((2, 3, 32, 512), BF16),
             pltpu.VMEM((32, 512), BF16),
             pltpu.VMEM((32, 512), BF16),
-            pltpu.SemaphoreType.DMA((5,)),
+            pltpu.SemaphoreType.DMA((6,)),
             pltpu.SemaphoreType.DMA((n,)),
             pltpu.SemaphoreType.DMA((n,)),
         ],

time: 60.1 us -> 57.5 us (0.957)
  the two profiles are of different devices: /device:TPU:1 before, /device:TPU:25 now
where the time goes in v2:
time: 57.5 us; the launch traced here: 57.3 us
  Pallas kernels  55.9 us (97%)
  local copies, waits for them, and re-layouts  1.38 us (2%)
    pallas_call x1, Pallas kernels, shards(): pl.pallas_call(kernel, out_shape=jax.ShapeDtypeStruct((32, 512), BF16), i...  55.9 us
    unnamed x1, local copies, waits for them, and re-layouts  1.38 us

profile of v2, /device:TPU:25, one launch (start us, length us, event | category | flops | bytes accessed | tf_op | source)
XLA Modules:
  0.0 57.3 jit_solution(9681064534744509502)
XLA Ops:
  0.0 55.9 %shard_map.64 = bf16[32,512]{1,0:T(8,128)(2,1)} custom-call(bf16[32,512]{1,0:T(8,128)(2,1)} %feat_hbm.1, s32[6,16,1,1024]{3,2,1,0:T(1,128)} %adj_hbm.1, s32[6,4,32]{2,1,0:T(4,128)} %bitcast.3, bf16[256,512]{1,0:T(8,128)(2,1)} %bitcast.2, f32[6,8]{1,0:T(8,128)} %coef_hbm.1, bf16[32,512]{1,0:T(8,128)(2,1)} %self_hbm.1), custom_call_target="tpu_custom_call" | custom-call | tf_op jit(solution)/shard_map/pallas_call | solution.py:301
  55.9 1.4 %copy.8 = bf16[32,512]{1,0:T(8,128)(2,1)} copy(bf16[32,512]{1,0:T(8,128)(2,1)} %shard_map.64) | data formatting | bytes 65536
